TPU v7x, 512 devices: a whole 4x8x8 slice. The times are simulated.
512 devices in a mesh: row: 32 (over x, y_lo, core), col: 16 (over y_hi, z).
Axes of the slice: x: 4, y: 8 (y_hi: 2, y_lo: 4; y = y_hi * 4 + y_lo), z: 8, core: 2. Of those that a mesh axis runs over, the one named last changes fastest.
Arguments:
- object_slices: float32 [2, 2, 4096, 2048], P(None, None, 'row', 'col'), may hold values from -5 to 5
- probe: float32 [2, 256, 256], replicated, may hold values from -6 to 6
- offsets: int32 [32, 16, 1, 2], P('row', 'col'), may hold values from 0 to 127
- residuals: float32 [32, 16, 1, 2, 256, 256], P('row', 'col'), may hold values from -6 to 6
Outputs:
- new_object: float32 [2, 2, 4096, 2048], P(None, None, 'row', 'col')
All inputs are finite; a program needn't handle non-finite values.
Results may differ from a plain program's by a relative error of at most 0.0003.
Values sent between devices are 32-bit elements; how exact they have to be, the bound alone decides.
A program may use at most 64 MiB of HBM per device.

v0:
```python
from functools import partial
import math

import jax
import jax.numpy as jnp
from jax import lax
from jax.sharding import PartitionSpec as P

FRESNEL = 40.0
STEP_SIZE = 0.5
REGULAR = 1.0


def passed_along(value, axis, steps):
    count = lax.axis_size(axis)
    pairs = [(source, (source + steps) % count) for source in range(count)]
    return lax.ppermute(value, axis, pairs)


def complex_dot(left_re, left_im, right_re, right_im):
    matmul = partial(jnp.dot, precision=lax.Precision.HIGHEST, preferred_element_type=jnp.float32)
    return (
        matmul(left_re, right_re) - matmul(left_im, right_im),
        matmul(left_re, right_im) + matmul(left_im, right_re),
    )


def sandwich(mat_re, mat_im, wave_re, wave_im):
    inner_re, inner_im = complex_dot(mat_re, mat_im, wave_re, wave_im)
    return complex_dot(inner_re, inner_im, mat_re, mat_im)


def tables(width):
    index = jnp.arange(width, dtype=jnp.int32)
    product = index[:, None] * index[None, :] % width
    angle = 2.0 * math.pi / width * product.astype(jnp.float32)
    factor = 1.0 / math.sqrt(width)
    four_re = jnp.cos(angle) * factor
    four_im = -jnp.sin(angle) * factor
    freq = jnp.where(index < width // 2, index, index - width).astype(jnp.float32) / width
    phase = FRESNEL * math.pi * freq * freq
    kern_re = jnp.cos(phase)
    kern_im = -jnp.sin(phase)
    scaled_re = four_re * kern_re[None, :] + four_im * kern_im[None, :]
    scaled_im = four_re * kern_im[None, :] - four_im * kern_re[None, :]
    prop_re, prop_im = complex_dot(scaled_re, scaled_im, four_re, four_im)
    return (four_re, four_im, prop_re, prop_im)


def one_position(window, probe, resid, four_re, four_im, prop_re, prop_im):
    layers = window.shape[0]
    wave_re, wave_im = (probe[0], probe[1])
    waves = [(wave_re, wave_im)]
    layer = 0
    trans_re = window[layer, 0]
    trans_im = window[layer, 1]
    exit_re = wave_re * trans_re - wave_im * trans_im
    exit_im = wave_re * trans_im + wave_im * trans_re
    wave_re, wave_im = sandwich(prop_re, prop_im, exit_re, exit_im)
    waves.append((wave_re, wave_im))
    back_re, back_im = sandwich(four_re, -four_im, resid[0], resid[1])
    parts = [None] * layers
    for layer in reversed(range(layers)):
        wave_re, wave_im = waves[layer]
        parts[layer] = jnp.stack(
            [
                wave_re * back_re + wave_im * back_im,
                wave_re * back_im - wave_im * back_re,
                wave_re * wave_re + wave_im * wave_im,
            ]
        )
        if layer > 0:
            trans_re, trans_im = (window[layer, 0], window[layer, 1])
            pulled_re = trans_re * back_re + trans_im * back_im
            pulled_im = trans_re * back_im - trans_im * back_re
            back_re, back_im = sandwich(prop_re, -prop_im, pulled_re, pulled_im)
    return jnp.stack(parts)


def rows_pass(buffer):
    third = buffer.shape[2] // 3
    strips = [buffer[:, :, band * third : (band + 1) * third] for band in range(3)]
    total = strips[2]
    for band in (1, 0):
        total = passed_along(total, "row", 1) + strips[band]
    return total


def cols_pass(buffer):
    third = buffer.shape[3] // 3
    strips = [buffer[:, :, :, band * third : (band + 1) * third] for band in range(3)]
    total = strips[2]
    for band in (1, 0):
        total = passed_along(total, "col", 1) + strips[band]
    return total


def build_region(object_slices):
    pieces = [object_slices]
    current = object_slices
    for band in range(2):
        current = passed_along(current, "row", -1)
        pieces.append(current)
    column = jnp.concatenate(pieces, axis=2)
    pieces = [column]
    current = column
    for band in range(2):
        current = passed_along(current, "col", -1)
        pieces.append(current)
    return jnp.concatenate(pieces, axis=3)


def local(object_slices, probe, offsets, residuals):
    layers = object_slices.shape[0]
    width = probe.shape[1]
    region = build_region(object_slices)
    four_re, four_im, prop_re, prop_im = tables(width)
    buffer = jnp.zeros((layers, 3, region.shape[2], region.shape[3]), jnp.float32)
    zero = jnp.zeros((), jnp.int32)
    top = offsets[0, 0, 0, 0]
    left = offsets[0, 0, 0, 1]
    window = lax.dynamic_slice(region, (zero, zero, top, left), (layers, 2, width, width))
    contrib = one_position(window, probe, residuals[0, 0, 0], four_re, four_im, prop_re, prop_im)
    older = lax.dynamic_slice(buffer, (zero, zero, top, left), (layers, 3, width, width))
    buffer = lax.dynamic_update_slice(buffer, older + contrib, (zero, zero, top, left))
    gathered = cols_pass(rows_pass(buffer))
    gradient = gathered[:, 0:2]
    illumination = gathered[:, 2:3]
    return object_slices - STEP_SIZE * gradient / (illumination + REGULAR)


def solution(mesh):
    placed = (
        P(None, None, "row", "col"),
        P(),
        P("row", "col", None, None),
        P("row", "col", None, None, None, None),
    )
    return jax.shard_map(
        local, mesh=mesh, in_specs=placed, out_specs=P(None, None, "row", "col"), check_vma=False
    )
```

profile of v0, /device:TPU:6, one launch (start us, length us, event | category | flops | bytes accessed | tf_op | source)
XLA Modules:
  0.0 233.8 jit_solution(9031556436662477619)
XLA Ops:
  0.0 5.3 %collective-permute-start = (f32[2,2,128,128]{3,2,1,0:T(8,128)}, f32[2,2,128,128]{3,2,1,0:T(8,128)S(1)}, u32[]{:S(2)}, u32[]{:S(2)}) collective-permute-start(f32[2,2,128,128]{3,2,1,0:T(8,128)} %param.4), channel_id=1, source_target_pairs={{0,496},{16,0},{32,16},{48,32},{64,48},{80,64},{96,80},{112,96},{1... | collective-permute-start | bytes 786440 | tf_op jit(solution)/shard_map/ppermute | solution.py:17
  5.3 3.0 %fusion.13 = f32[256,256]{1,0:T(8,128)} fusion(f32[1,1,1,2,256,256]{5,4,3,2,1,0:T(8,128)} %param.7), kind=kOutput, calls=%fused_computation.49 | convolution fusion | flops 202309632 | bytes 524288 | tf_op jit(solution)/shard_map/dot_general | solution.py:24
  8.4 1.4 fusion.17
  9.7 1.4 convolution_subtract_fusion.5
  11.2 2.1 fusion.42
  13.2 2.7 %collective-permute-start.1 = (f32[2,2,128,128]{3,2,1,0:T(8,128)S(1)}, f32[2,2,128,128]{3,2,1,0:T(8,128)S(1)}, u32[]{:S(2)}, u32[]{:S(2)}) collective-permute-start(f32[2,2,128,128]{3,2,1,0:T(8,128)S(1)} %collective-permute-done), channel_id=1, source_target_pairs={{0,496},{16,0},{32,16},{48,32},{64,48},{80,64},{96,80},{112,96},{1... | collective-permute-start | bytes 786440 | tf_op jit(solution)/shard_map/ppermute | solution.py:17
  15.9 1.5 fusion.26
  17.5 2.3 collective-permute-done.1
  19.8 13.7 %collective-permute-start.2 = (f32[2,2,384,128]{3,2,1,0:T(8,128)S(1)}, f32[2,2,384,128]{3,2,1,0:T(8,128)S(1)}, u32[]{:S(2)}, u32[]{:S(2)}) collective-permute-start(f32[2,2,384,128]{3,2,1,0:T(8,128)S(1)} %constant_dynamic-update-slice_fusion), channel_id=1, source_target_pairs={{0,15},{1,0},{2,1},{3,2},{4,3},{5,4},{6,5},{7,6},{8,7},{9,8},{10,9... | collective-permute-start | bytes 2359304 | tf_op jit(solution)/shard_map/ppermute | solution.py:17
  33.5 2.2 fusion.40
  35.7 2.1 fusion.37
  37.8 1.5 convolution_add_fusion.4
  39.3 19.2 %collective-permute-done.2 = f32[2,2,384,128]{3,2,1,0:T(8,128)S(1)} collective-permute-done((f32[2,2,384,128]{3,2,1,0:T(8,128)S(1)}, f32[2,2,384,128]{3,2,1,0:T(8,128)S(1)}, u32[]{:S(2)}, u32[]{:S(2)}) %collective-permute-start.2) | collective-permute-done | bytes 786464 | tf_op jit(solution)/shard_map/ppermute | solution.py:17
  58.5 19.5 %collective-permute-start.3 = (f32[2,2,384,128]{3,2,1,0:T(8,128)S(1)}, f32[2,2,384,128]{3,2,1,0:T(8,128)S(1)}, u32[]{:S(2)}, u32[]{:S(2)}) collective-permute-start(f32[2,2,384,128]{3,2,1,0:T(8,128)S(1)} %collective-permute-done.2), channel_id=1, source_target_pairs={{0,15},{1,0},{2,1},{3,2},{4,3},{5,4},{6,5},{7,6},{8,7},{9,8},{10,9... | collective-permute-start | bytes 2359304 | tf_op jit(solution)/shard_map/ppermute | solution.py:17
  77.9 0.6 fusion.130
  82.4 2.5 %convolution_subtract_fusion.6 = f32[256,256]{1,0:T(8,128)S(1)} fusion(f32[256,256]{1,0:T(8,128)} %fusion.40, f32[256]{0:T(256)S(1)} %get-tuple-element.19, f32[256]{0:T(256)S(1)} %get-tuple-element.20), kind=kOutput, calls=%fused_computation.19 | convolution fusion | flops 203620352 | bytes 526336 | tf_op jit(solution)/shard_map/dot_general | solution.py:23
  84.9 1.4 convolution_add_fusion.6
  86.3 1.4 convolution_add_fusion.5
  87.7 24.1 %collective-permute-done.3 = f32[2,2,384,128]{3,2,1,0:T(8,128)S(1)} collective-permute-done((f32[2,2,384,128]{3,2,1,0:T(8,128)S(1)}, f32[2,2,384,128]{3,2,1,0:T(8,128)S(1)}, u32[]{:S(2)}, u32[]{:S(2)}) %collective-permute-start.3) | collective-permute-done | bytes 786464 | tf_op jit(solution)/shard_map/ppermute | solution.py:17
  111.8 0.8 fusion.1
  112.6 1.4 multiply_subtract_fusion
  114.0 0.4 fusion.135
  114.4 0.4 fusion.133
  114.8 0.4 convolution_subtract_fusion.3
  115.2 0.4 fusion.29
  115.6 0.4 fusion.134
  116.0 0.4 fusion.136
  116.3 0.4 fusion.138
  116.7 0.4 convolution_subtract_fusion.1
  117.1 0.4 fusion.139
  117.5 0.4 fusion.137
  117.9 0.4 convolution_add_fusion.3
  118.3 0.4 convolution_add_fusion.1
  118.7 0.4 convolution_add_fusion
  119.1 0.4 convolution_subtract_fusion
  119.4 0.6 convolution_add_fusion.2
  120.1 0.4 fusion.8
  120.7 1.3 pad_maximum_fusion
  122.2 20.5 %dynamic_update_slice.3 = f32[2,3,384,384]{3,2,1,0:T(8,128)S(1)} dynamic-update-slice(f32[2,3,384,384]{3,2,1,0:T(8,128)S(1)} %broadcast_in_dim.2, f32[2,3,256,256]{3,2,1,0:T(8,128)} %pad_maximum_fusion, s32[]{:T(128)} %constant.14.clone.1, s32[]{:T(128)} %constant.14.clone.1, s32[]{:T(128)S(6)} %select_n.64, s32[]{:T(128)S(6)} %select_n.65) | dynamic-update-slice | bytes 3145732 | tf_op jit(solution)/shard_map/dynamic_update_slice | solution.py:125
  142.8 1.9 collective-permute-start.4
  144.8 18.3 %collective-permute-done.4 = f32[2,3,128,384]{3,2,1,0:T(8,128)S(1)} collective-permute-done((f32[2,3,128,384]{3,2,1,0:T(8,128)S(1)}, f32[2,3,128,384]{3,2,1,0:T(8,128)S(1)}, u32[]{:S(2)}, u32[]{:S(2)}) %collective-permute-start.4) | collective-permute-done | bytes 1179680 | tf_op jit(solution)/shard_map/ppermute | solution.py:17
  163.2 1.9 collective-permute-start.5
  165.2 18.3 %collective-permute-done.5 = f32[2,3,128,384]{3,2,1,0:T(8,128)S(1)} collective-permute-done((f32[2,3,128,384]{3,2,1,0:T(8,128)S(1)}, f32[2,3,128,384]{3,2,1,0:T(8,128)S(1)}, u32[]{:S(2)}, u32[]{:S(2)}) %collective-permute-start.5) | collective-permute-done | bytes 1179680 | tf_op jit(solution)/shard_map/ppermute | solution.py:17
  183.7 2.1 collective-permute-start.6
  185.7 31.5 %collective-permute-done.6 = f32[2,3,128,128]{3,2,1,0:T(8,128)S(1)} collective-permute-done((f32[2,3,128,128]{3,2,1,0:T(8,128)S(1)}, f32[2,3,128,128]{3,2,1,0:T(8,128)S(1)}, u32[]{:S(2)}, u32[]{:S(2)}) %collective-permute-start.6) | collective-permute-done | bytes 393248 | tf_op jit(solution)/shard_map/ppermute | solution.py:17
  217.3 1.9 collective-permute-start.7
  219.3 13.8 %collective-permute-done.7 = f32[2,3,128,128]{3,2,1,0:T(8,128)S(1)} collective-permute-done((f32[2,3,128,128]{3,2,1,0:T(8,128)S(1)}, f32[2,3,128,128]{3,2,1,0:T(8,128)S(1)}, u32[]{:S(2)}, u32[]{:S(2)}) %collective-permute-start.7) | collective-permute-done | bytes 393248 | tf_op jit(solution)/shard_map/ppermute | solution.py:17
  233.1 0.7 fusion.6
  (35 shorter events, 1.2 us)
Async XLA Ops:
  0.0 8.4 %copy-start.5 = (f32[1,1,1,2,256,256]{5,4,3,2,1,0:T(8,128)S(1)}, f32[1,1,1,2,256,256]{5,4,3,2,1,0:T(8,128)}, u32[]{:S(2)}) copy-start(f32[1,1,1,2,256,256]{5,4,3,2,1,0:T(8,128)} %param.7) | copy-start | bytes 1572868
  0.0 13.2 %collective-permute-start = (f32[2,2,128,128]{3,2,1,0:T(8,128)}, f32[2,2,128,128]{3,2,1,0:T(8,128)S(1)}, u32[]{:S(2)}, u32[]{:S(2)}) collective-permute-start(f32[2,2,128,128]{3,2,1,0:T(8,128)} %param.4), channel_id=1, source_target_pairs={{0,496},{16,0},{32,16},{48,32},{64,48},{80,64},{96,80},{112,96},{1... | collective-permute-start | bytes 786440 | tf_op jit(solution)/shard_map/ppermute | solution.py:17
  13.2 6.6 %collective-permute-start.1 = (f32[2,2,128,128]{3,2,1,0:T(8,128)S(1)}, f32[2,2,128,128]{3,2,1,0:T(8,128)S(1)}, u32[]{:S(2)}, u32[]{:S(2)}) collective-permute-start(f32[2,2,128,128]{3,2,1,0:T(8,128)S(1)} %collective-permute-done), channel_id=1, source_target_pairs={{0,496},{16,0},{32,16},{48,32},{64,48},{80,64},{96,80},{112,96},{1... | collective-permute-start | bytes 786440 | tf_op jit(solution)/shard_map/ppermute | solution.py:17
  15.9 1.5 copy-start.1
  19.8 38.6 %collective-permute-start.2 = (f32[2,2,384,128]{3,2,1,0:T(8,128)S(1)}, f32[2,2,384,128]{3,2,1,0:T(8,128)S(1)}, u32[]{:S(2)}, u32[]{:S(2)}) collective-permute-start(f32[2,2,384,128]{3,2,1,0:T(8,128)S(1)} %constant_dynamic-update-slice_fusion), channel_id=1, source_target_pairs={{0,15},{1,0},{2,1},{3,2},{4,3},{5,4},{6,5},{7,6},{8,7},{9,8},{10,9... | collective-permute-start | bytes 2359304 | tf_op jit(solution)/shard_map/ppermute | solution.py:17
  35.7 2.1 copy-start
  37.8 40.1 %copy-start.4 = (s32[1,1,1,2]{3,2,1,0:T(1,128)S(1)}, s32[1,1,1,2]{3,2,1,0:T(1,128)}, u32[]{:S(2)}) copy-start(s32[1,1,1,2]{3,2,1,0:T(1,128)} %param.6) | copy-start | bytes 28
  58.5 53.3 %collective-permute-start.3 = (f32[2,2,384,128]{3,2,1,0:T(8,128)S(1)}, f32[2,2,384,128]{3,2,1,0:T(8,128)S(1)}, u32[]{:S(2)}, u32[]{:S(2)}) collective-permute-start(f32[2,2,384,128]{3,2,1,0:T(8,128)S(1)} %collective-permute-done.2), channel_id=1, source_target_pairs={{0,15},{1,0},{2,1},{3,2},{4,3},{5,4},{6,5},{7,6},{8,7},{9,8},{10,9... | collective-permute-start | bytes 2359304 | tf_op jit(solution)/shard_map/ppermute | solution.py:17
  82.4 2.5 %copy-start.6 = (f32[1,1,1,2,256,256]{5,4,3,2,1,0:T(8,128)S(1)}, f32[1,1,1,2,256,256]{5,4,3,2,1,0:T(8,128)}, u32[]{:S(2)}) copy-start(f32[1,1,1,2,256,256]{5,4,3,2,1,0:T(8,128)} %param.7) | copy-start | bytes 1572868
  82.4 2.5 %copy-start.8 = (f32[256,256]{1,0:T(8,128)S(1)}, f32[256,256]{1,0:T(8,128)}, u32[]{:S(2)}) copy-start(f32[256,256]{1,0:T(8,128)} %fusion.13) | copy-start | bytes 786436
  84.9 1.4 copy-start.7
  87.7 24.9 %copy-start.3 = (f32[256,256]{1,0:T(8,128)S(1)}, f32[256,256]{1,0:T(8,128)}, u32[]{:S(2)}) copy-start(f32[256,256]{1,0:T(8,128)} %fusion.37) | copy-start | bytes 786436
  142.8 20.2 %collective-permute-start.4 = (f32[2,3,128,384]{3,2,1,0:T(8,128)S(1)}, f32[2,3,128,384]{3,2,1,0:T(8,128)S(1)}, u32[]{:S(2)}, u32[]{:S(2)}) collective-permute-start(f32[2,3,128,384]{3,2,1,0:T(8,128)S(1)} %slice.78), channel_id=1, source_target_pairs={{0,16},{16,32},{32,48},{48,64},{64,80},{80,96},{96,112},{112,128},... | collective-permute-start | bytes 3538952 | tf_op jit(solution)/shard_map/ppermute | solution.py:17
  163.2 20.2 %collective-permute-start.5 = (f32[2,3,128,384]{3,2,1,0:T(8,128)S(1)}, f32[2,3,128,384]{3,2,1,0:T(8,128)S(1)}, u32[]{:S(2)}, u32[]{:S(2)}) collective-permute-start(f32[2,3,128,384]{3,2,1,0:T(8,128)S(1)} %slice_add_fusion.1), channel_id=1, source_target_pairs={{0,16},{16,32},{32,48},{48,64},{64,80},{80,96},{96,112},{112,128},... | collective-permute-start | bytes 3538952 | tf_op jit(solution)/shard_map/ppermute | solution.py:17
  183.7 49.4 %copy-start.2 = (f32[2,2,128,128]{3,2,1,0:T(8,128)S(1)}, f32[2,2,128,128]{3,2,1,0:T(8,128)}, u32[]{:S(2)}) copy-start(f32[2,2,128,128]{3,2,1,0:T(8,128)} %param.4) | copy-start | bytes 786436
  183.7 33.6 %collective-permute-start.6 = (f32[2,3,128,128]{3,2,1,0:T(8,128)S(1)}, f32[2,3,128,128]{3,2,1,0:T(8,128)S(1)}, u32[]{:S(2)}, u32[]{:S(2)}) collective-permute-start(f32[2,3,128,128]{3,2,1,0:T(8,128)S(1)} %slice.81), channel_id=1, source_target_pairs={{0,1},{1,2},{2,3},{3,4},{4,5},{5,6},{6,7},{7,8},{8,9},{9,10},{10,1... | collective-permute-start | bytes 1179656 | tf_op jit(solution)/shard_map/ppermute | solution.py:17
  217.3 15.7 %collective-permute-start.7 = (f32[2,3,128,128]{3,2,1,0:T(8,128)S(1)}, f32[2,3,128,128]{3,2,1,0:T(8,128)S(1)}, u32[]{:S(2)}, u32[]{:S(2)}) collective-permute-start(f32[2,3,128,128]{3,2,1,0:T(8,128)S(1)} %slice_add_fusion.3), channel_id=1, source_target_pairs={{0,1},{1,2},{2,3},{3,4},{4,5},{5,6},{6,7},{7,8},{8,9},{9,10},{10,1... | collective-permute-start | bytes 1179656 | tf_op jit(solution)/shard_map/ppermute | solution.py:17
where the time goes:
time: 236 us; the launch traced here: 234 us
  waiting for transfers between devices  127 us (54%)
  starting transfers between devices  49 us (21%)
  matrix products  28 us (12%)
  local copies, waits for them, and re-layouts  21.6 us (9%)
  between operations  4.22 us (2%)
  other arithmetic  3.56 us (2%)
    ppermute x8, waiting for transfers between devices, passed_along(): return lax.ppermute(value, axis, pairs)  127 us
    ppermute x8, starting transfers between devices, passed_along(): return lax.ppermute(value, axis, pairs)  49 us
    dynamic_update_slice x1, local copies, waits for them, and re-layouts, local(): lax.dynamic_update_slice(buffer, older + contrib, (zero, zero, top, left))  20.5 us
    dot_general x7, matrix products, complex_dot(): matmul(left_re, right_im) + matmul(left_im, right_re)  8.07 us
    dot_general x7, matrix products, complex_dot(): matmul(left_re, right_re) - matmul(left_im, right_im)  7.11 us
    dot_general x7, matrix products, complex_dot(): matmul(left_im, right_im)  6.86 us
    dot_general x7, matrix products, complex_dot(): matmul(left_im, right_re)  5.95 us
  transfers between devices with their start and end apart: 8, of which 7 were waited for; matrix products, arithmetic and copies ran while one was open for 9% of the time, Pallas kernels for 0%

commit v1 on v0

v1 whole, which is shorter than its diff:
```python
import math

import jax
import jax.numpy as jnp
import numpy as np
from jax import lax
from jax.experimental import pallas as pl
from jax.experimental.pallas import tpu as pltpu
from jax.sharding import PartitionSpec as P

FRESNEL = 40.0
STEP_SIZE = 0.5
REGULAR = 1.0
MESH = pl.DeviceIdType.MESH
F32 = jnp.float32
BF16 = jnp.bfloat16


def halves(mat):
    high = mat.astype(jnp.bfloat16)
    low = (mat - high.astype(np.float64)).astype(jnp.bfloat16)
    return [high, low]


def tables(width):
    index = np.arange(width)
    angle = 2.0 * math.pi / width * ((index[:, None] * index[None, :]) % width)
    inverse = np.exp(1j * angle) / math.sqrt(width)
    freq = np.where(index < width // 2, index, index - width) / width
    kern = np.exp(-1j * FRESNEL * math.pi * freq * freq)
    prop = (inverse * kern[None, :]) @ np.conj(inverse)
    pack = lambda mat: np.stack(halves(mat.real) + halves(mat.imag))
    return pack(inverse), pack(prop)


def split(value):
    high = value.astype(BF16)
    return high, (value - high.astype(F32)).astype(BF16)


def dot(left, right):
    return jnp.dot(left, right, preferred_element_type=F32)


def names():
    found = {}
    for kind, count in (("z1", 1), ("z2", 1), ("a", 3), ("b", 3), ("f", 3), ("q1", 3), ("q2", 3), ("q3", 3), ("c2", 1), ("c1", 1)):
        for layer in range(2):
            for band in range(count):
                found[kind, layer, band] = len(found)
    return found


SLOTS = names()


def kernel(
    n_row, n_col, offs, obj, probe, resid, ftab, atab, out,
    reg, work, four_r, four_l, prop_r, prop_l, half, psi0, back1, terms, rx_a, rx_b, rx_c, rx_d, tx, ssem, rsem,
):
    tile = obj.shape[2]
    width = 2 * tile
    row = lax.axis_index("row")
    col = lax.axis_index("col")
    odd = lax.rem(row, 2) == 1
    even = lax.rem(row, 2) == 0
    at = lambda dr, dc: (lax.rem(row + dr + n_row, n_row), lax.rem(col + dc + n_col, n_col))

    barrier = pltpu.get_barrier_semaphore()
    greet = lambda who: pl.semaphore_signal(barrier, inc=1, device_id=who, device_id_type=MESH)
    for who in (at(0, -1), at(0, 1), at(-1, 0), at(1, 0)):
        greet(who)

    @pl.when(odd)
    def _():
        greet(at(-2, 0))
        greet(at(2, 0))
        pl.semaphore_wait(barrier, 6)

    @pl.when(even)
    def _():
        pl.semaphore_wait(barrier, 4)

    def copy(kind, layer, band, source, target, who):
        slot = SLOTS[kind, layer, band]
        return pltpu.make_async_remote_copy(
            src_ref=source, dst_ref=target, send_sem=ssem.at[slot], recv_sem=rsem.at[slot], device_id=who, device_id_type=MESH
        )

    own = lambda s, j: obj.at[s] if j == 0 else reg.at[s, 0, j]
    z1 = lambda s: copy("z1", s, 0, obj.at[s], reg.at[s, 0, 1], at(0, -1))
    z2 = lambda s: copy("z2", s, 0, reg.at[s, 0, 1], reg.at[s, 0, 2], at(0, -1))
    step_a = lambda s, j: copy("a", s, j, own(s, j), reg.at[s, 1, j], at(-1, 0))
    step_b = lambda s, j: copy("b", s, j, own(s, j), reg.at[s, 2, j], at(-2, 0))
    step_f = lambda s, j: copy("f", s, j, reg.at[s, 1, j], reg.at[s, 2, j], at(-1, 0))
    q1 = lambda s, j: copy("q1", s, j, terms.at[s, 1, j], rx_a.at[s, j], at(1, 0))
    q1s = lambda s, j: copy("q1", s, j, tx.at[s, j], rx_a.at[s, j], at(1, 0))
    q2 = lambda s, j: copy("q2", s, j, terms.at[s, 2, j], rx_b.at[s, j], at(2, 0))
    q3 = lambda s, j: copy("q3", s, j, terms.at[s, 2, j], rx_c.at[s, j], at(1, 0))
    c2 = lambda s: copy("c2", s, 0, tx.at[s, 3], rx_d.at[s, 0], at(0, 1))
    c1 = lambda s: copy("c1", s, 0, tx.at[s, 4], rx_d.at[s, 1], at(0, 1))

    def strip(s, j):
        step_a(s, j).start()

        @pl.when(odd)
        def _():
            step_b(s, j).start()

    for s in range(2):
        z1(s).start()
        strip(s, 0)

    top = offs[0]
    left = offs[1]

    def mirrored(plain_re, plain_im, right, part):
        neg = -plain_im
        if right:
            part[0:width, 0:width] = plain_re
            part[0:width, width:] = plain_im
            part[width:, 0:width] = neg
            part[width:, width:] = plain_re
        else:
            part[0:width, 0:width] = plain_re
            part[0:width, width:] = neg
            part[width:, 0:width] = plain_im
            part[width:, width:] = plain_re

    for k in range(2):
        mirrored(atab[k], atab[2 + k], True, prop_r.at[k])
        mirrored(atab[k], atab[2 + k], False, prop_l.at[k])

    def one_hot(shift, axis):
        place = lax.broadcasted_iota(jnp.int32, (width, width), axis)
        other = lax.broadcasted_iota(jnp.int32, (width, width), 1 - axis)
        moved = place - shift
        moved = jnp.where(moved < 0, moved + width, moved)
        return jnp.where(moved == other, 1.0, 0.0).astype(BF16)

    rows_hot = one_hot(top, 0)
    cols_hot = one_hot(left, 1)
    for k in range(2):
        mirrored(dot(ftab[k], cols_hot).astype(BF16), dot(ftab[2 + k], cols_hot).astype(BF16), True, four_r.at[k])
        mirrored(dot(rows_hot, ftab[k]).astype(BF16), dot(rows_hot, ftab[2 + k]).astype(BF16), False, four_l.at[k])

    for k in range(2):
        total = None
        for part in split(probe[k]):
            moved = dot(dot(rows_hot, part).astype(BF16), cols_hot)
            total = moved if total is None else total + moved
        psi0[k] = total

    def put(k, rows, cols, value):
        high, low = split(value)
        base = k * width
        work[0, rows, base + cols.start : base + cols.stop] = high
        work[1, rows, base + cols.start : base + cols.stop] = low

    def sandwich(left_mat, right_mat):
        inner = dot(work[0], right_mat[0]) + (dot(work[1], right_mat[0]) + dot(work[0], right_mat[1]))
        for k in range(2):
            high, low = split(inner[:, k * width : (k + 1) * width])
            half[0, k * width : (k + 1) * width, :] = high
            half[1, k * width : (k + 1) * width, :] = low
        return dot(left_mat[0], half[0]) + (dot(left_mat[1], half[0]) + dot(left_mat[0], half[1]))

    everything = slice(0, width)
    for k in range(2):
        put(k, everything, everything, resid[k])
    both = sandwich(four_l, four_r)
    back1[0] = both[0:width]
    back1[1] = both[width:]

    rowm = lax.broadcasted_iota(jnp.int32, (tile, tile), 0) >= top
    colm = lax.broadcasted_iota(jnp.int32, (tile, tile), 1) >= left
    lo = slice(0, tile)
    hi = slice(tile, width)

    def piece(s, i, j, k):
        return obj[s, k] if i == 0 and j == 0 else reg[s, i, j, k]

    def quadrant(s, rows, cols, k):
        if rows is lo and cols is lo:
            return jnp.where(
                rowm,
                jnp.where(colm, piece(s, 0, 0, k), piece(s, 0, 2, k)),
                jnp.where(colm, piece(s, 2, 0, k), piece(s, 2, 2, k)),
            )
        if rows is lo:
            return jnp.where(rowm, piece(s, 0, 1, k), piece(s, 2, 1, k))
        if cols is lo:
            return jnp.where(colm, piece(s, 1, 0, k), piece(s, 1, 2, k))
        return piece(s, 1, 1, k)

    def scatter(s, ch, value):
        zero = jnp.zeros((tile, tile), F32)
        corner = value[lo, lo]
        upper = jnp.where(rowm, corner, zero)
        lower = jnp.where(rowm, zero, corner)
        terms[s, 0, 0, ch] = jnp.where(colm, upper, zero)
        terms[s, 0, 2, ch] = jnp.where(colm, zero, upper)
        terms[s, 2, 0, ch] = jnp.where(colm, lower, zero)
        terms[s, 2, 2, ch] = jnp.where(colm, zero, lower)
        corner = value[lo, hi]
        terms[s, 0, 1, ch] = jnp.where(rowm, corner, zero)
        terms[s, 2, 1, ch] = jnp.where(rowm, zero, corner)
        corner = value[hi, lo]
        terms[s, 1, 0, ch] = jnp.where(colm, corner, zero)
        terms[s, 1, 2, ch] = jnp.where(colm, zero, corner)
        terms[s, 1, 1, ch] = value[hi, hi]

    def arrivals(s):
        for j in range(3):
            step_a(s, j).wait_recv()

            @pl.when(odd)
            def _():
                step_f(s, j).start()

        for j in range(3):

            @pl.when(odd)
            def _():
                step_b(s, j).wait_recv()

            @pl.when(even)
            def _():
                step_f(s, j).wait_recv()

    for s in range(2):
        z1(s).wait_recv()
        z2(s).start()
        strip(s, 1)
    for s in range(2):
        z2(s).wait_recv()
        strip(s, 2)

    def send_terms(s):
        for j in (2, 1, 0):

            @pl.when(odd)
            def _():
                q2(s, j).start()

            @pl.when(even)
            def _():
                q3(s, j).start()
                q1(s, j).start()

    def send_sums(s):
        for j in (2, 1, 0):

            @pl.when(odd)
            def _():
                q3(s, j).wait_recv()
                tx[s, j] = terms[s, 1, j] + rx_c[s, j]
                q1s(s, j).start()

    def row_total(s, j):
        q1(s, j).wait_recv()

        @pl.when(odd)
        def _():
            q2(s, j).wait_recv()

        @pl.when(odd)
        def _():
            terms[s, 0, j] = terms[s, 0, j] + (rx_a[s, j] + rx_b[s, j])

        @pl.when(even)
        def _():
            terms[s, 0, j] = terms[s, 0, j] + rx_a[s, j]

        return terms[s, 0, j]

    arrivals(0)
    for rows in (lo, hi):
        for cols in (lo, hi):
            obj_re, obj_im = quadrant(0, rows, cols, 0), quadrant(0, rows, cols, 1)
            psi_re, psi_im = psi0[0, rows, cols], psi0[1, rows, cols]
            put(0, rows, cols, psi_re * obj_re - psi_im * obj_im)
            put(1, rows, cols, psi_re * obj_im + psi_im * obj_re)
    both = sandwich(prop_l, prop_r)
    wave_re, wave_im = both[0:width], both[width:]
    scatter(1, 0, wave_re * back1[0] + wave_im * back1[1])
    scatter(1, 1, wave_re * back1[1] - wave_im * back1[0])
    scatter(1, 2, wave_re * wave_re + wave_im * wave_im)
    send_terms(1)

    arrivals(1)
    for rows in (lo, hi):
        for cols in (lo, hi):
            obj_re, obj_im = quadrant(1, rows, cols, 0), quadrant(1, rows, cols, 1)
            back_re, back_im = back1[0, rows, cols], back1[1, rows, cols]
            put(0, rows, cols, obj_re * back_re + obj_im * back_im)
            put(1, rows, cols, obj_im * back_re - obj_re * back_im)
    send_sums(1)
    both = sandwich(prop_l, prop_r)
    conj_re, conj_im = both[0:width], both[width:]
    scatter(0, 0, psi0[0] * conj_re - psi0[1] * conj_im)
    scatter(0, 1, -(psi0[0] * conj_im + psi0[1] * conj_re))
    scatter(0, 2, psi0[0] * psi0[0] + psi0[1] * psi0[1])
    send_terms(0)

    tx[1, 3] = row_total(1, 2)
    c2(1).start()
    send_sums(0)
    middle = row_total(1, 1)
    c2(1).wait_recv()
    tx[1, 4] = middle + rx_d[1, 0]
    c1(1).start()
    tx[0, 3] = row_total(0, 2)
    c2(0).start()
    middle = row_total(0, 1)
    c2(0).wait_recv()
    tx[0, 4] = middle + rx_d[0, 0]
    c1(0).start()
    for s in (1, 0):
        last = row_total(s, 0)
        c1(s).wait_recv()
        total = last + rx_d[s, 1]
        scale = STEP_SIZE / (total[2] + REGULAR)
        for k in range(2):
            out[s, k] = obj[s, k] - total[k] * scale

    for s in range(2):
        for sent in (z1(s), z2(s), c2(s), c1(s)):
            sent.wait_send()
        for j in range(3):
            step_a(s, j).wait_send()
            q1(s, j).wait_send()

            @pl.when(odd)
            def _():
                step_b(s, j).wait_send()
                step_f(s, j).wait_send()
                q2(s, j).wait_send()

            @pl.when(even)
            def _():
                q3(s, j).wait_send()


def solution(mesh):
    n_row, n_col = mesh.shape["row"], mesh.shape["col"]

    def local(object_slices, probe, offsets, residuals):
        layers, parts, tile, _ = object_slices.shape
        width = probe.shape[1]
        four, prop = tables(width)
        vmem = pl.BlockSpec(memory_space=pltpu.VMEM)
        stack = pltpu.VMEM((2, 2 * width, 2 * width), BF16)
        block = (3, tile, tile)
        call = pl.pallas_call(
            lambda *refs: kernel(n_row, n_col, *refs),
            out_shape=jax.ShapeDtypeStruct(object_slices.shape, F32),
            in_specs=[pl.BlockSpec(memory_space=pltpu.SMEM)] + [vmem] * 5,
            out_specs=vmem,
            scratch_shapes=[
                pltpu.VMEM((layers, 3, 3, parts, tile, tile), F32),
                pltpu.VMEM((2, width, 2 * width), BF16),
                stack, stack, stack, stack,
                pltpu.VMEM((2, 2 * width, width), BF16),
                pltpu.VMEM((2, width, width), F32),
                pltpu.VMEM((2, width, width), F32),
                pltpu.VMEM((layers, 3, 3) + block, F32),
                pltpu.VMEM((layers, 3) + block, F32),
                pltpu.VMEM((layers, 3) + block, F32),
                pltpu.VMEM((layers, 3) + block, F32),
                pltpu.VMEM((layers, 2) + block, F32),
                pltpu.VMEM((layers, 5) + block, F32),
                pltpu.SemaphoreType.DMA((len(SLOTS),)),
                pltpu.SemaphoreType.DMA((len(SLOTS),)),
            ],
            compiler_params=pltpu.CompilerParams(collective_id=0, has_side_effects=True, vmem_limit_bytes=56 * 1024 * 1024),
            name="ptycho",
        )
        return call(offsets.reshape(2), object_slices, probe, residuals[0, 0, 0], jnp.asarray(four), jnp.asarray(prop))

    placed = (
        P(None, None, "row", "col"),
        P(),
        P("row", "col", None, None),
        P("row", "col", None, None, None, None),
    )
    return jax.shard_map(local, mesh=mesh, in_specs=placed, out_specs=P(None, None, "row", "col"), check_vma=False)
```

time: 236 us -> 156 us (0.66)
  the two profiles are of different devices: /device:TPU:6 before, /device:TPU:5 now
where the time goes in v1:
time: 156 us
  Pallas kernels  154 us (99%)
  local copies, waits for them, and re-layouts  1.67 us (1%)
    pallas_call x1, Pallas kernels, local(): call(offsets.reshape(2), object_slices, probe, residuals[0, 0, 0], jnp.as...  154 us

profile of v1, /device:TPU:5, one launch (start us, length us, event | category | flops | bytes accessed | tf_op | source)
XLA Modules:
  0.0 155.8 jit_solution(4621594166752514989)
XLA Ops:
  0.0 154.1 %ptycho.1 = f32[2,2,128,128]{3,2,1,0:T(8,128)} custom-call(s32[2]{0:T(128)} %bitcast.3, f32[2,2,128,128]{3,2,1,0:T(8,128)} %refs_1_.1, f32[2,256,256]{2,1,0:T(8,128)} %refs_2_.1, f32[2,256,256]{2,1,0:T(8,128)} %bitcast.2, bf16[4,256,256]{2,1,0:T(8,128)(2,1)} %constant.4.clone.refs_4_, bf16[4,256,256]{2,1,0:T(8,128)(2,1)} %constant.5.clone.refs_5_), custom_call_target="tpu_custom_call" | custom-call | tf_op jit(solution)/shard_map/ptycho/pallas_call | solution.py:379
  154.1 1.7 %copy.8 = f32[2,2,128,128]{3,2,1,0:T(8,128)} copy(f32[2,2,128,128]{3,2,1,0:T(8,128)} %ptycho.1) | data formatting | bytes 524288

commit v2 on v1

--- a/solution.py
+++ b/solution.py
@@ -42,12 +42,30 @@
     return jnp.dot(left, right, preferred_element_type=F32)
 
 
+GATHER_PARTS = (
+    (0, 64, ((0, 0), (1, 7))),
+    (64, 128, ((0, 0), (0, 7), (1, 7))),
+)
+SUM_PARTS = (
+    (0, 64, ((0, 7), (1, 0))),
+    (64, 128, ((0, 7), (0, 0), (1, 0))),
+)
+
+
 def names():
     found = {}
-    for kind, count in (("z1", 1), ("z2", 1), ("a", 3), ("b", 3), ("f", 3), ("q1", 3), ("q2", 3), ("q3", 3), ("c2", 1), ("c1", 1)):
+    kinds = (("z1", 1), ("z2", 1), ("a", 3), ("b", 3), ("f", 3), ("q1", 3), ("q2", 3), ("q3", 3), ("c2", 1), ("c1", 1))
+    for kind, count in kinds:
         for layer in range(2):
             for band in range(count):
                 found[kind, layer, band] = len(found)
+    for kind in ("z1", "z2", "c2", "c1"):
+        for layer in range(2):
+            for k, part in enumerate(GATHER_PARTS if kind[0] == "z" else SUM_PARTS):
+                for leg in range(len(part[2]) - 1):
+                    found[kind, layer, (k, leg)] = len(found)
+    for band in range(4):
+        found["o", 0, band] = len(found)
     return found
 
 
@@ -56,7 +74,7 @@
 
 def kernel(
     n_row, n_col, offs, obj, probe, resid, ftab, atab, out,
-    reg, work, four_r, four_l, prop_r, prop_l, half, psi0, back1, terms, rx_a, rx_b, rx_c, rx_d, tx, ssem, rsem,
+    reg, work, four_r, four_l, prop_r, prop_l, half, psi0, back1, terms, rx_a, rx_b, rx_c, rx_d, tx, relay_z, relay_c, places, row_hot, col_hot, picked, light0, ssem, rsem,
 ):
     tile = obj.shape[2]
     width = 2 * tile
@@ -66,20 +84,42 @@
     even = lax.rem(row, 2) == 0
     at = lambda dr, dc: (lax.rem(row + dr + n_row, n_row), lax.rem(col + dc + n_col, n_col))
 
+    depth = n_col // 2
+    plane = lax.rem(col, depth)
+    base = col - plane
+    flipped = depth - base
+    top = offs[0]
+    left = offs[1]
+    line = lax.broadcasted_iota(jnp.int32, places.shape[2:], 0)
+    places[0, 0] = jnp.where(line == 0, top, left).astype(F32)
+
     barrier = pltpu.get_barrier_semaphore()
     greet = lambda who: pl.semaphore_signal(barrier, inc=1, device_id=who, device_id_type=MESH)
-    for who in (at(0, -1), at(0, 1), at(-1, 0), at(1, 0)):
+    for who in (at(0, -1), at(0, 1), at(0, -2), at(0, 2), at(-1, 0), at(1, 0), at(-2, 0), at(2, 0)):
         greet(who)
-
-    @pl.when(odd)
-    def _():
-        greet(at(-2, 0))
-        greet(at(2, 0))
-        pl.semaphore_wait(barrier, 6)
-
-    @pl.when(even)
-    def _():
-        pl.semaphore_wait(barrier, 4)
+    count = 8
+    hops = []
+    for parts in (GATHER_PARTS, SUM_PARTS):
+        for _, _, path in parts:
+            for leg in range(len(path) - 1):
+                if len(path) > 2:
+                    hops.append((path[leg], path[leg + 1]))
+
+    def place_of(node, other):
+        return (row, (base if node[0] == other[0] else flipped) + other[1])
+
+    for first, second in hops:
+
+        @pl.when(plane == first[1])
+        def _():
+            greet(place_of(first, second))
+
+        @pl.when(plane == second[1])
+        def _():
+            greet(place_of(second, first))
+
+        count = count + jnp.where(plane == first[1], 1, 0) + jnp.where(plane == second[1], 1, 0)
+    pl.semaphore_wait(barrier, count)
 
     def copy(kind, layer, band, source, target, who):
         slot = SLOTS[kind, layer, band]
@@ -87,18 +127,87 @@
             src_ref=source, dst_ref=target, send_sem=ssem.at[slot], recv_sem=rsem.at[slot], device_id=who, device_id_type=MESH
         )
 
+    class Message:
+        def __init__(self, kind, layer, source, target, relay, parts, step):
+            self.first, self.last = parts[0][2][0][1], parts[0][2][-1][1]
+            self.main = copy(kind, layer, 0, source, target, at(0, step))
+            self.legs = []
+            for k, (low, high, path) in enumerate(parts):
+                here = source.at[:, low:high]
+                for leg in range(len(path) - 1):
+                    final = leg == len(path) - 2
+                    there = target.at[:, low:high] if final else relay.at[leg, :, low:high]
+                    who = place_of(path[leg], path[leg + 1])
+                    self.legs.append((path[leg][1], path[leg + 1][1], leg == 0, final, copy(kind, layer, (k, leg), here, there, who)))
+                    here = there
+
+        def start(self):
+            @pl.when(plane != self.first)
+            def _():
+                self.main.start()
+
+            @pl.when(plane == self.first)
+            def _():
+                for _, _, opening, _, leg in self.legs:
+                    if opening:
+                        leg.start()
+
+        def relay(self):
+            for k, (_, sink, _, final, leg) in enumerate(self.legs):
+                if not final:
+                    following = self.legs[k + 1][4]
+
+                    @pl.when(plane == sink)
+                    def _():
+                        leg.wait_recv()
+                        following.start()
+
+        def wait_recv(self):
+            @pl.when(plane != self.last)
+            def _():
+                self.main.wait_recv()
+
+            self.relay()
+
+            @pl.when(plane == self.last)
+            def _():
+                for _, _, _, final, leg in self.legs:
+                    if final:
+                        leg.wait_recv()
+
+        def wait_send(self):
+            @pl.when(plane != self.first)
+            def _():
+                self.main.wait_send()
+
+            for source, _, _, _, leg in self.legs:
+
+                @pl.when(plane == source)
+                def _():
+                    leg.wait_send()
+
     own = lambda s, j: obj.at[s] if j == 0 else reg.at[s, 0, j]
-    z1 = lambda s: copy("z1", s, 0, obj.at[s], reg.at[s, 0, 1], at(0, -1))
-    z2 = lambda s: copy("z2", s, 0, reg.at[s, 0, 1], reg.at[s, 0, 2], at(0, -1))
+    z1_all = [Message("z1", s, obj.at[s], reg.at[s, 0, 1], relay_z.at[s, 0], GATHER_PARTS, -1) for s in range(2)]
+    z2_all = [Message("z2", s, reg.at[s, 0, 1], reg.at[s, 0, 2], relay_z.at[s, 1], GATHER_PARTS, -1) for s in range(2)]
+    z1 = lambda s: z1_all[s]
+    z2 = lambda s: z2_all[s]
     step_a = lambda s, j: copy("a", s, j, own(s, j), reg.at[s, 1, j], at(-1, 0))
     step_b = lambda s, j: copy("b", s, j, own(s, j), reg.at[s, 2, j], at(-2, 0))
     step_f = lambda s, j: copy("f", s, j, reg.at[s, 1, j], reg.at[s, 2, j], at(-1, 0))
-    q1 = lambda s, j: copy("q1", s, j, terms.at[s, 1, j], rx_a.at[s, j], at(1, 0))
-    q1s = lambda s, j: copy("q1", s, j, tx.at[s, j], rx_a.at[s, j], at(1, 0))
-    q2 = lambda s, j: copy("q2", s, j, terms.at[s, 2, j], rx_b.at[s, j], at(2, 0))
-    q3 = lambda s, j: copy("q3", s, j, terms.at[s, 2, j], rx_c.at[s, j], at(1, 0))
-    c2 = lambda s: copy("c2", s, 0, tx.at[s, 3], rx_d.at[s, 0], at(0, 1))
-    c1 = lambda s: copy("c1", s, 0, tx.at[s, 4], rx_d.at[s, 1], at(0, 1))
+    full = lambda s: slice(0, 2 + s)
+    q1 = lambda s, j: copy("q1", s, j, terms.at[s, 1, j, full(s)], rx_a.at[s, j, full(s)], at(1, 0))
+    q1s = lambda s, j: copy("q1", s, j, tx.at[s, j, full(s)], rx_a.at[s, j, full(s)], at(1, 0))
+    q2 = lambda s, j: copy("q2", s, j, terms.at[s, 2, j, full(s)], rx_b.at[s, j, full(s)], at(2, 0))
+    q3 = lambda s, j: copy("q3", s, j, terms.at[s, 2, j, full(s)], rx_c.at[s, j, full(s)], at(1, 0))
+    sums = lambda kind, s, k: Message(
+        kind, s, tx.at[s, 3 + k, full(s)], rx_d.at[s, k, full(s)], relay_c.at[s, k, :, full(s)], SUM_PARTS, 1
+    )
+    c2_all = [sums("c2", s, 0) for s in range(2)]
+    c1_all = [sums("c1", s, 1) for s in range(2)]
+    c2 = lambda s: c2_all[s]
+    c1 = lambda s: c1_all[s]
+    near = [copy("o", 0, i - 1, places.at[0, 0], places.at[0, i], at(i, 0)) for i in (1, 2)]
+    far = [copy("o", 0, j + 1, places.at[0], places.at[j], at(0, j)) for j in (1, 2)]
 
     def strip(s, j):
         step_a(s, j).start()
@@ -107,12 +216,11 @@
         def _():
             step_b(s, j).start()
 
+    for sent in near:
+        sent.start()
     for s in range(2):
         z1(s).start()
         strip(s, 0)
-
-    top = offs[0]
-    left = offs[1]
 
     def mirrored(plain_re, plain_im, right, part):
         neg = -plain_im
@@ -228,6 +336,10 @@
             def _():
                 step_f(s, j).wait_recv()
 
+    for sent in near:
+        sent.wait_recv()
+    for sent in far:
+        sent.start()
     for s in range(2):
         z1(s).wait_recv()
         z2(s).start()
@@ -254,7 +366,7 @@
             @pl.when(odd)
             def _():
                 q3(s, j).wait_recv()
-                tx[s, j] = terms[s, 1, j] + rx_c[s, j]
+                tx[s, j, full(s)] = terms[s, 1, j, full(s)] + rx_c[s, j, full(s)]
                 q1s(s, j).start()
 
     def row_total(s, j):
@@ -266,13 +378,13 @@
 
         @pl.when(odd)
         def _():
-            terms[s, 0, j] = terms[s, 0, j] + (rx_a[s, j] + rx_b[s, j])
+            terms[s, 0, j, full(s)] = terms[s, 0, j, full(s)] + (rx_a[s, j, full(s)] + rx_b[s, j, full(s)])
 
         @pl.when(even)
         def _():
-            terms[s, 0, j] = terms[s, 0, j] + rx_a[s, j]
-
-        return terms[s, 0, j]
+            terms[s, 0, j, full(s)] = terms[s, 0, j, full(s)] + rx_a[s, j, full(s)]
+
+        return terms[s, 0, j, full(s)]
 
     arrivals(0)
     for rows in (lo, hi):
@@ -288,6 +400,36 @@
     scatter(1, 2, wave_re * wave_re + wave_im * wave_im)
     send_terms(1)
 
+    send_sums(1)
+    for sent in far:
+        sent.wait_recv()
+    light = split(probe[0] * probe[0] + probe[1] * probe[1])
+    across = lax.broadcasted_iota(jnp.int32, (tile, tile), 1).astype(F32)
+    down = lax.broadcasted_iota(jnp.int32, (tile, tile), 0).astype(F32)
+    for i in range(3):
+        for j in range(3):
+            spot = (3 * j + i) * tile
+            shift = places[j, i, 0:1, :]
+            for k in range(2):
+                hit = down + float(tile * (i - k)) - shift == across
+                row_hot[spot : spot + tile, k * tile : (k + 1) * tile] = jnp.where(hit, 1.0, 0.0).astype(BF16)
+            shift = places[j, i, 1:2, :]
+            for k in range(2):
+                hit = across + float(tile * (j - k)) - shift == down
+                col_hot[3 * j + i, k * tile : (k + 1) * tile, :] = jnp.where(hit, 1.0, 0.0).astype(BF16)
+    total = jnp.zeros((tile, tile), F32)
+    for part in light:
+        picked[...] = dot(row_hot[...], part).astype(BF16)
+        for k in range(9):
+            total = total + dot(picked[k * tile : (k + 1) * tile, :], col_hot[k])
+    light0[...] = total
+
+    tx[1, 3, full(1)] = row_total(1, 2)
+    c2(1).start()
+    middle = row_total(1, 1)
+    c2(1).wait_recv()
+    tx[1, 4, full(1)] = middle + rx_d[1, 0, full(1)]
+    c1(1).start()
     arrivals(1)
     for rows in (lo, hi):
         for cols in (lo, hi):
@@ -295,35 +437,29 @@
             back_re, back_im = back1[0, rows, cols], back1[1, rows, cols]
             put(0, rows, cols, obj_re * back_re + obj_im * back_im)
             put(1, rows, cols, obj_im * back_re - obj_re * back_im)
-    send_sums(1)
     both = sandwich(prop_l, prop_r)
     conj_re, conj_im = both[0:width], both[width:]
     scatter(0, 0, psi0[0] * conj_re - psi0[1] * conj_im)
     scatter(0, 1, -(psi0[0] * conj_im + psi0[1] * conj_re))
-    scatter(0, 2, psi0[0] * psi0[0] + psi0[1] * psi0[1])
     send_terms(0)
 
-    tx[1, 3] = row_total(1, 2)
-    c2(1).start()
     send_sums(0)
-    middle = row_total(1, 1)
-    c2(1).wait_recv()
-    tx[1, 4] = middle + rx_d[1, 0]
-    c1(1).start()
-    tx[0, 3] = row_total(0, 2)
+    tx[0, 3, full(0)] = row_total(0, 2)
     c2(0).start()
     middle = row_total(0, 1)
     c2(0).wait_recv()
-    tx[0, 4] = middle + rx_d[0, 0]
+    tx[0, 4, full(0)] = middle + rx_d[0, 0, full(0)]
     c1(0).start()
     for s in (1, 0):
         last = row_total(s, 0)
         c1(s).wait_recv()
-        total = last + rx_d[s, 1]
-        scale = STEP_SIZE / (total[2] + REGULAR)
+        total = last + rx_d[s, 1, full(s)]
+        scale = STEP_SIZE / ((total[2] if s == 1 else light0[...]) + REGULAR)
         for k in range(2):
             out[s, k] = obj[s, k] - total[k] * scale
 
+    for sent in near + far:
+        sent.wait_send()
     for s in range(2):
         for sent in (z1(s), z2(s), c2(s), c1(s)):
             sent.wait_send()
@@ -370,6 +506,13 @@
                 pltpu.VMEM((layers, 3) + block, F32),
                 pltpu.VMEM((layers, 2) + block, F32),
                 pltpu.VMEM((layers, 5) + block, F32),
+                pltpu.VMEM((layers, 2, 2, parts, tile, tile), F32),
+                pltpu.VMEM((layers, 2, 2) + block, F32),
+                pltpu.VMEM((3, 3, 8, tile), F32),
+                pltpu.VMEM((9 * tile, width), BF16),
+                pltpu.VMEM((9, width, tile), BF16),
+                pltpu.VMEM((9 * tile, width), BF16),
+                pltpu.VMEM((tile, tile), F32),
                 pltpu.SemaphoreType.DMA((len(SLOTS),)),
                 pltpu.SemaphoreType.DMA((len(SLOTS),)),
             ],

time: 156 us -> 123 us (0.79)
  the two profiles are of different devices: /device:TPU:5 before, /device:TPU:20 now
where the time goes in v2:
time: 123 us
  Pallas kernels  121 us (98%)
  local copies, waits for them, and re-layouts  1.67 us (1%)
    pallas_call x1, Pallas kernels, local(): call(offsets.reshape(2), object_slices, probe, residuals[0, 0, 0], jnp.as...  121 us

profile of v2, /device:TPU:20, one launch (start us, length us, event | category | flops | bytes accessed | tf_op | source)
XLA Modules:
  0.0 122.9 jit_solution(7468620577887829393)
XLA Ops:
  0.0 121.2 %ptycho.1 = f32[2,2,128,128]{3,2,1,0:T(8,128)} custom-call(s32[2]{0:T(128)} %bitcast.3, f32[2,2,128,128]{3,2,1,0:T(8,128)} %refs_1_.1, f32[2,256,256]{2,1,0:T(8,128)} %refs_2_.1, f32[2,256,256]{2,1,0:T(8,128)} %bitcast.2, bf16[4,256,256]{2,1,0:T(8,128)(2,1)} %constant.4.clone.refs_4_, bf16[4,256,256]{2,1,0:T(8,128)(2,1)} %constant.5.clone.refs_5_), custom_call_target="tpu_custom_call" | custom-call | tf_op jit(solution)/shard_map/ptycho/pallas_call | solution.py:522
  121.2 1.7 %copy.8 = f32[2,2,128,128]{3,2,1,0:T(8,128)} copy(f32[2,2,128,128]{3,2,1,0:T(8,128)} %ptycho.1) | data formatting | bytes 524288

commit v3 on v2

--- a/solution.py
+++ b/solution.py
@@ -43,13 +43,14 @@
 
 
 GATHER_PARTS = (
-    (0, 64, ((0, 0), (1, 7))),
-    (64, 128, ((0, 0), (0, 7), (1, 7))),
+    (0, 88, ((0, 0), (1, 7))),
+    (88, 128, ((0, 0), (0, 7), (1, 7))),
 )
 SUM_PARTS = (
-    (0, 64, ((0, 7), (1, 0))),
-    (64, 128, ((0, 7), (0, 0), (1, 0))),
+    ((0, 72, ((0, 7), (1, 0))), (72, 128, ((0, 7), (0, 0), (1, 0)))),
+    ((0, 56, ((0, 7), (1, 0))), (56, 128, ((0, 7), (0, 0), (1, 0)))),
 )
+REROUTES = (((0, 1), (1, 0)), ((0, 2), (1, 1)), ((7, 0), (6, 1)))
 
 
 def names():
@@ -61,9 +62,14 @@
                 found[kind, layer, band] = len(found)
     for kind in ("z1", "z2", "c2", "c1"):
         for layer in range(2):
-            for k, part in enumerate(GATHER_PARTS if kind[0] == "z" else SUM_PARTS):
+            for k, part in enumerate(GATHER_PARTS if kind[0] == "z" else SUM_PARTS[layer]):
                 for leg in range(len(part[2]) - 1):
                     found[kind, layer, (k, leg)] = len(found)
+    for kind in ("e", "g"):
+        for layer in range(2):
+            for k in range(len(REROUTES)):
+                for i in (1, 2):
+                    found[kind, layer, (i, k)] = len(found)
     for band in range(4):
         found["o", 0, band] = len(found)
     return found
@@ -74,7 +80,7 @@
 
 def kernel(
     n_row, n_col, offs, obj, probe, resid, ftab, atab, out,
-    reg, work, four_r, four_l, prop_r, prop_l, half, psi0, back1, terms, rx_a, rx_b, rx_c, rx_d, tx, relay_z, relay_c, places, row_hot, col_hot, picked, light0, ssem, rsem,
+    reg, work, four_r, four_l, prop_r, prop_l, half, psi0, back1, terms, rx_a, rx_b, rx_c, rx_d, rx_e, tx, relay_z, relay_c, places, row_hot, col_hot, picked, light0, ssem, rsem,
 ):
     tile = obj.shape[2]
     width = 2 * tile
@@ -99,7 +105,7 @@
         greet(who)
     count = 8
     hops = []
-    for parts in (GATHER_PARTS, SUM_PARTS):
+    for parts in (GATHER_PARTS, SUM_PARTS[0]):
         for _, _, path in parts:
             for leg in range(len(path) - 1):
                 if len(path) > 2:
@@ -200,7 +206,7 @@
     q2 = lambda s, j: copy("q2", s, j, terms.at[s, 2, j, full(s)], rx_b.at[s, j, full(s)], at(2, 0))
     q3 = lambda s, j: copy("q3", s, j, terms.at[s, 2, j, full(s)], rx_c.at[s, j, full(s)], at(1, 0))
     sums = lambda kind, s, k: Message(
-        kind, s, tx.at[s, 3 + k, full(s)], rx_d.at[s, k, full(s)], relay_c.at[s, k, :, full(s)], SUM_PARTS, 1
+        kind, s, tx.at[s, 3 + k, full(s)], rx_d.at[s, k, full(s)], relay_c.at[s, k, :, full(s)], SUM_PARTS[s], 1
     )
     c2_all = [sums("c2", s, 0) for s in range(2)]
     c1_all = [sums("c1", s, 1) for s in range(2)]
@@ -209,12 +215,36 @@
     near = [copy("o", 0, i - 1, places.at[0, 0], places.at[0, i], at(i, 0)) for i in (1, 2)]
     far = [copy("o", 0, j + 1, places.at[0], places.at[j], at(0, j)) for j in (1, 2)]
 
+    def on(choices):
+        found = plane < 0
+        for choice in choices:
+            found = found | (plane == choice)
+        return found
+
+    taken = [on([take[0] for take, _ in REROUTES if take[1] == j]) for j in range(3)]
+    given = [on([give[0] for _, give in REROUTES if give[1] == j]) for j in range(3)]
+    kept = [jnp.logical_not(which) for which in taken]
+    takes = lambda j: [(k, odd & (plane == take[0])) for k, (take, _) in enumerate(REROUTES) if take[1] == j]
+    gives = lambda j: [(k, odd & (plane == give[0])) for k, (_, give) in enumerate(REROUTES) if give[1] == j]
+
+    def step_e(s, i, k):
+        (to_plane, to_band), (from_plane, from_band) = REROUTES[k]
+        return copy("e", s, (i, k), reg.at[s, i, from_band], reg.at[s, i, to_band], at(0, to_plane - from_plane))
+
+    def step_g(s, i, k):
+        (to_plane, to_band), (from_plane, _) = REROUTES[k]
+        source = tx.at[s, to_band, full(s)] if i == 1 else terms.at[s, 2, to_band, full(s)]
+        return copy("g", s, (i, k), source, rx_e.at[s, i - 1, k, full(s)], at(0, from_plane - to_plane))
+
+    def when(condition, *acts):
+        @pl.when(condition)
+        def _():
+            for act in acts:
+                act()
+
     def strip(s, j):
-        step_a(s, j).start()
-
-        @pl.when(odd)
-        def _():
-            step_b(s, j).start()
+        when(odd | kept[j], step_a(s, j).start)
+        when(odd & kept[j], step_b(s, j).start)
 
     for sent in near:
         sent.start()
@@ -320,21 +350,19 @@
 
     def arrivals(s):
         for j in range(3):
-            step_a(s, j).wait_recv()
-
-            @pl.when(odd)
-            def _():
-                step_f(s, j).start()
-
+            when(even | kept[j], step_a(s, j).wait_recv)
+            for k, here in takes(j):
+                when(here, step_e(s, 1, k).wait_recv)
+            when(odd, step_f(s, j).start)
+            for k, here in gives(j):
+                when(here, step_e(s, 1, k).start)
+            when(odd & kept[j], step_b(s, j).wait_recv)
+            for k, here in takes(j):
+                when(here, step_e(s, 2, k).wait_recv)
+            for k, here in gives(j):
+                when(here, step_e(s, 2, k).start)
         for j in range(3):
-
-            @pl.when(odd)
-            def _():
-                step_b(s, j).wait_recv()
-
-            @pl.when(even)
-            def _():
-                step_f(s, j).wait_recv()
+            when(even, step_f(s, j).wait_recv)
 
     for sent in near:
         sent.wait_recv()
@@ -350,15 +378,10 @@
 
     def send_terms(s):
         for j in (2, 1, 0):
-
-            @pl.when(odd)
-            def _():
-                q2(s, j).start()
-
-            @pl.when(even)
-            def _():
-                q3(s, j).start()
-                q1(s, j).start()
+            when(odd & kept[j] & jnp.logical_not(given[j]), q2(s, j).start)
+            for k, here in takes(j):
+                when(here, step_g(s, 2, k).start)
+            when(even, q3(s, j).start, q1(s, j).start)
 
     def send_sums(s):
         for j in (2, 1, 0):
@@ -367,23 +390,33 @@
             def _():
                 q3(s, j).wait_recv()
                 tx[s, j, full(s)] = terms[s, 1, j, full(s)] + rx_c[s, j, full(s)]
-                q1s(s, j).start()
+
+            for k, here in gives(j):
+
+                @pl.when(here)
+                def _():
+                    step_g(s, 2, k).wait_recv()
+                    terms[s, 2, j, full(s)] = terms[s, 2, j, full(s)] + rx_e[s, 1, k, full(s)]
+                    q2(s, j).start()
+                    step_g(s, 1, k).wait_recv()
+                    tx[s, j, full(s)] = tx[s, j, full(s)] + rx_e[s, 0, k, full(s)]
+
+            when(odd & kept[j], q1s(s, j).start)
+            for k, here in takes(j):
+                when(here, step_g(s, 1, k).start)
 
     def row_total(s, j):
-        q1(s, j).wait_recv()
-
-        @pl.when(odd)
-        def _():
-            q2(s, j).wait_recv()
-
-        @pl.when(odd)
-        def _():
-            terms[s, 0, j, full(s)] = terms[s, 0, j, full(s)] + (rx_a[s, j, full(s)] + rx_b[s, j, full(s)])
-
-        @pl.when(even)
-        def _():
-            terms[s, 0, j, full(s)] = terms[s, 0, j, full(s)] + rx_a[s, j, full(s)]
-
+        when(even & kept[j] | odd, q1(s, j).wait_recv)
+        when(odd & kept[j], q2(s, j).wait_recv)
+
+        def add(*others):
+            total = terms[s, 0, j, full(s)]
+            for other in others:
+                total = total + other[s, j, full(s)]
+            terms[s, 0, j, full(s)] = total
+
+        when(odd & kept[j], lambda: add(rx_a, rx_b))
+        when(even & kept[j] | odd & taken[j], lambda: add(rx_a))
         return terms[s, 0, j, full(s)]
 
     arrivals(0)
@@ -399,6 +432,14 @@
     scatter(1, 1, wave_re * back1[1] - wave_im * back1[0])
     scatter(1, 2, wave_re * wave_re + wave_im * wave_im)
     send_terms(1)
+
+    def pass_columns(s):
+        tx[s, 3, full(s)] = row_total(s, 2)
+        c2(s).start()
+        middle = row_total(s, 1)
+        c2(s).wait_recv()
+        tx[s, 4, full(s)] = middle + rx_d[s, 0, full(s)]
+        c1(s).start()
 
     send_sums(1)
     for sent in far:
@@ -424,12 +465,8 @@
             total = total + dot(picked[k * tile : (k + 1) * tile, :], col_hot[k])
     light0[...] = total
 
-    tx[1, 3, full(1)] = row_total(1, 2)
-    c2(1).start()
-    middle = row_total(1, 1)
-    c2(1).wait_recv()
-    tx[1, 4, full(1)] = middle + rx_d[1, 0, full(1)]
-    c1(1).start()
+    when(plane == depth - 1, lambda: pass_columns(1))
+
     arrivals(1)
     for rows in (lo, hi):
         for cols in (lo, hi):
@@ -443,13 +480,10 @@
     scatter(0, 1, -(psi0[0] * conj_im + psi0[1] * conj_re))
     send_terms(0)
 
+    when((plane != depth - 1) & (plane != 0), lambda: pass_columns(1))
     send_sums(0)
-    tx[0, 3, full(0)] = row_total(0, 2)
-    c2(0).start()
-    middle = row_total(0, 1)
-    c2(0).wait_recv()
-    tx[0, 4, full(0)] = middle + rx_d[0, 0, full(0)]
-    c1(0).start()
+    when(plane == 0, lambda: pass_columns(1))
+    pass_columns(0)
     for s in (1, 0):
         last = row_total(s, 0)
         c1(s).wait_recv()
@@ -464,18 +498,15 @@
         for sent in (z1(s), z2(s), c2(s), c1(s)):
             sent.wait_send()
         for j in range(3):
-            step_a(s, j).wait_send()
-            q1(s, j).wait_send()
-
-            @pl.when(odd)
-            def _():
-                step_b(s, j).wait_send()
-                step_f(s, j).wait_send()
-                q2(s, j).wait_send()
-
-            @pl.when(even)
-            def _():
-                q3(s, j).wait_send()
+            when(odd | kept[j], step_a(s, j).wait_send)
+            when(even | kept[j], q1(s, j).wait_send)
+            when(odd & kept[j], step_b(s, j).wait_send, q2(s, j).wait_send)
+            when(odd, step_f(s, j).wait_send)
+            when(even, q3(s, j).wait_send)
+            for k, here in gives(j):
+                when(here, step_e(s, 1, k).wait_send, step_e(s, 2, k).wait_send)
+            for k, here in takes(j):
+                when(here, step_g(s, 1, k).wait_send, step_g(s, 2, k).wait_send)
 
 
 def solution(mesh):
@@ -505,6 +536,7 @@
                 pltpu.VMEM((layers, 3) + block, F32),
                 pltpu.VMEM((layers, 3) + block, F32),
                 pltpu.VMEM((layers, 2) + block, F32),
+                pltpu.VMEM((layers, 2, len(REROUTES)) + block, F32),
                 pltpu.VMEM((layers, 5) + block, F32),
                 pltpu.VMEM((layers, 2, 2, parts, tile, tile), F32),
                 pltpu.VMEM((layers, 2, 2) + block, F32),

time: 123 us -> 104 us (0.85)
  the two profiles are of different devices: /device:TPU:20 before, /device:TPU:26 now
where the time goes in v3:
time: 104 us
  Pallas kernels  103 us (99%)
  local copies, waits for them, and re-layouts  1.67 us (2%)
    pallas_call x1, Pallas kernels, local(): call(offsets.reshape(2), object_slices, probe, residuals[0, 0, 0], jnp.as...  103 us

profile of v3, /device:TPU:26, one launch (start us, length us, event | category | flops | bytes accessed | tf_op | source)
XLA Modules:
  0.0 104.3 jit_solution(16826030757353837946)
XLA Ops:
  0.0 102.6 %ptycho.1 = f32[2,2,128,128]{3,2,1,0:T(8,128)} custom-call(s32[2]{0:T(128)} %bitcast.3, f32[2,2,128,128]{3,2,1,0:T(8,128)} %refs_1_.1, f32[2,256,256]{2,1,0:T(8,128)} %refs_2_.1, f32[2,256,256]{2,1,0:T(8,128)} %bitcast.2, bf16[4,256,256]{2,1,0:T(8,128)(2,1)} %constant.4.clone.refs_4_, bf16[4,256,256]{2,1,0:T(8,128)(2,1)} %constant.5.clone.refs_5_), custom_call_target="tpu_custom_call" | custom-call | tf_op jit(solution)/shard_map/ptycho/pallas_call | solution.py:554
  102.6 1.7 %copy.8 = f32[2,2,128,128]{3,2,1,0:T(8,128)} copy(f32[2,2,128,128]{3,2,1,0:T(8,128)} %ptycho.1) | data formatting | bytes 524288

commit v4 on v3

--- a/solution.py
+++ b/solution.py
@@ -47,8 +47,8 @@
     (88, 128, ((0, 0), (0, 7), (1, 7))),
 )
 SUM_PARTS = (
+    ((0, 80, ((0, 7), (1, 0))), (80, 128, ((0, 7), (0, 0), (1, 0)))),
     ((0, 72, ((0, 7), (1, 0))), (72, 128, ((0, 7), (0, 0), (1, 0)))),
-    ((0, 56, ((0, 7), (1, 0))), (56, 128, ((0, 7), (0, 0), (1, 0)))),
 )
 REROUTES = (((0, 1), (1, 0)), ((0, 2), (1, 1)), ((7, 0), (6, 1)))
 
@@ -433,14 +433,20 @@
     scatter(1, 2, wave_re * wave_re + wave_im * wave_im)
     send_terms(1)
 
-    def pass_columns(s):
+    def open_columns(s):
         tx[s, 3, full(s)] = row_total(s, 2)
         c2(s).start()
+
+    def close_columns(s):
         middle = row_total(s, 1)
         c2(s).wait_recv()
         tx[s, 4, full(s)] = middle + rx_d[s, 0, full(s)]
         c1(s).start()
 
+    giver = on([give[0] for _, give in REROUTES])
+    taker = on([take[0] for take, _ in REROUTES])
+    middle_planes = jnp.logical_not(taker)
+    when(giver, lambda: arrivals(1))
     send_sums(1)
     for sent in far:
         sent.wait_recv()
@@ -465,9 +471,10 @@
             total = total + dot(picked[k * tile : (k + 1) * tile, :], col_hot[k])
     light0[...] = total
 
-    when(plane == depth - 1, lambda: pass_columns(1))
-
-    arrivals(1)
+    when(taker, lambda: open_columns(1))
+    when(plane == depth - 1, lambda: close_columns(1))
+
+    when(jnp.logical_not(giver), lambda: arrivals(1))
     for rows in (lo, hi):
         for cols in (lo, hi):
             obj_re, obj_im = quadrant(1, rows, cols, 0), quadrant(1, rows, cols, 1)
@@ -480,10 +487,12 @@
     scatter(0, 1, -(psi0[0] * conj_im + psi0[1] * conj_re))
     send_terms(0)
 
-    when((plane != depth - 1) & (plane != 0), lambda: pass_columns(1))
+    when(middle_planes, lambda: open_columns(1))
+    when(middle_planes, lambda: close_columns(1))
     send_sums(0)
-    when(plane == 0, lambda: pass_columns(1))
-    pass_columns(0)
+    when(plane == 0, lambda: close_columns(1))
+    open_columns(0)
+    close_columns(0)
     for s in (1, 0):
         last = row_total(s, 0)
         c1(s).wait_recv()

time: 104 us -> 102 us (0.981)
  the two profiles are of different devices: /device:TPU:26 before, /device:TPU:6 now
where the time goes in v4:
time: 102 us
  Pallas kernels  100 us (98%)
  local copies, waits for them, and re-layouts  1.67 us (2%)
    pallas_call x1, Pallas kernels, local(): call(offsets.reshape(2), object_slices, probe, residuals[0, 0, 0], jnp.as...  100 us

profile of v4, /device:TPU:6, one launch (start us, length us, event | category | flops | bytes accessed | tf_op | source)
XLA Modules:
  0.0 101.9 jit_solution(12787530473113743773)
XLA Ops:
  0.0 100.2 %ptycho.1 = f32[2,2,128,128]{3,2,1,0:T(8,128)} custom-call(s32[2]{0:T(128)} %bitcast.3, f32[2,2,128,128]{3,2,1,0:T(8,128)} %refs_1_.1, f32[2,256,256]{2,1,0:T(8,128)} %refs_2_.1, f32[2,256,256]{2,1,0:T(8,128)} %bitcast.2, bf16[4,256,256]{2,1,0:T(8,128)(2,1)} %constant.4.clone.refs_4_, bf16[4,256,256]{2,1,0:T(8,128)(2,1)} %constant.5.clone.refs_5_), custom_call_target="tpu_custom_call" | custom-call | tf_op jit(solution)/shard_map/ptycho/pallas_call | solution.py:563
  100.2 1.7 %copy.8 = f32[2,2,128,128]{3,2,1,0:T(8,128)} copy(f32[2,2,128,128]{3,2,1,0:T(8,128)} %ptycho.1) | data formatting | bytes 524288

commit v5 on v4

--- a/solution.py
+++ b/solution.py
@@ -43,8 +43,8 @@
 
 
 GATHER_PARTS = (
-    (0, 88, ((0, 0), (1, 7))),
-    (88, 128, ((0, 0), (0, 7), (1, 7))),
+    (0, 96, ((0, 0), (1, 7))),
+    (96, 128, ((0, 0), (0, 7), (1, 7))),
 )
 SUM_PARTS = (
     ((0, 80, ((0, 7), (1, 0))), (80, 128, ((0, 7), (0, 0), (1, 0)))),

time: 102 us -> 102 us (level)
  no operation moved by 1% of the time
where the time goes in v5:
time: 102 us; the launch traced here: 101 us
  Pallas kernels  99.3 us (97%)
  local copies, waits for them, and re-layouts  1.67 us (2%)
    pallas_call x1, Pallas kernels, local(): call(offsets.reshape(2), object_slices, probe, residuals[0, 0, 0], jnp.as...  99.3 us

profile of v5, /device:TPU:6, one launch (start us, length us, event | category | flops | bytes accessed | tf_op | source)
XLA Modules:
  0.0 101.0 jit_solution(11490755020246038528)
XLA Ops:
  0.0 99.3 %ptycho.1 = f32[2,2,128,128]{3,2,1,0:T(8,128)} custom-call(s32[2]{0:T(128)} %bitcast.3, f32[2,2,128,128]{3,2,1,0:T(8,128)} %refs_1_.1, f32[2,256,256]{2,1,0:T(8,128)} %refs_2_.1, f32[2,256,256]{2,1,0:T(8,128)} %bitcast.2, bf16[4,256,256]{2,1,0:T(8,128)(2,1)} %constant.4.clone.refs_4_, bf16[4,256,256]{2,1,0:T(8,128)(2,1)} %constant.5.clone.refs_5_), custom_call_target="tpu_custom_call" | custom-call | tf_op jit(solution)/shard_map/ptycho/pallas_call | solution.py:563
  99.3 1.7 %copy.8 = f32[2,2,128,128]{3,2,1,0:T(8,128)} copy(f32[2,2,128,128]{3,2,1,0:T(8,128)} %ptycho.1) | data formatting | bytes 524288
